TPU v7x, 256 devices: a whole 4x4x8 slice. The times are simulated.
256 devices in a mesh: row: 128 (over y, z, x), grp: 2 (over core).
Axes of the slice: x: 4, y: 4, z: 8, core: 2. Of those that a mesh axis runs over, the one named last changes fastest.
Arguments:
- features: float32 [1048576, 256], P(('row', 'grp')), may hold values from -6 to 6
- session: int32 [1048576], P(('row', 'grp')), may hold values from 0 to 8191, never falling along the last dimension, each value on 1 to 163840 neighbouring positions
- owner_map: int32 [256, 64], P(('row', 'grp')), may hold values from 0 to 127, as said below
Outputs:
- received: bfloat16 [32768, 64, 256], P(('row', 'grp'))
Inputs may be any that keep to these rules, and one draw needn't show every extreme that they name: session numbers never fall along the rows; each session covers 1 to 163840 consecutive rows. `owner_map`: no owner is named by more than 1 of the blocks of one group of 64.
All inputs are finite; a program needn't handle non-finite values.
Results may differ from a plain program's by a relative error of at most 0.001.
Values may be sent and summed in bfloat16 or wider, within the bound.
A program may use at most 128 MiB of HBM per device.

v0:
```python
import jax
import jax.numpy as jnp
from jax import lax
from jax.experimental import pallas as pl
from jax.experimental.pallas import tpu as pltpu
from jax.sharding import Mesh
from jax.sharding import PartitionSpec as P

ROW = ("row_0", "row_1", "row_2")
ROW_GRP = ("row_0", "row_1", "row_2", "grp")
MOST = 163840
TILE = 128
ROOMS = ((35, 26, 17, 6), (36, 27, 18, 7), (37, 28, 19, 7), (40, 30, 21, 8), (56, 40, 24, 8))
MESH = pl.DeviceIdType.MESH


def coords(d, sizes):
    out = []
    for n in reversed(sizes):
        out.append(lax.rem(d, n))
        d = lax.div(d, n)
    return tuple(reversed(out))


def place():
    return tuple(lax.axis_index(name) for name in ROW_GRP)


def plane_order(y, x, nx):
    return lax.rem(x + y, nx) * nx + y


def prelude_kernel(
    sizes, reach, block_rows, slot_cap,
    owners_hbm, ids_hbm, feat_hbm,
    sums, cnt, open_out, unpack_out, pack_out, most_out,
    owners_ref, ids_ref, feat, ends, joins, tail, got, mine, got_line, top, got_plane,
    load_sem, send_sem, recv_sem, line_send, line_recv, plane_send, plane_recv,
):
    ny, nz, nx, ng = sizes
    devices = ny * nz * nx * ng
    me = lax.axis_index(ROW_GRP)
    y, z, x, g = place()
    rows_dev, width = feat.shape
    tiles = rows_dev // TILE
    blocks = rows_dev // block_rows
    line = nz * ng
    plane = ny * nx
    loads = [
        pltpu.make_async_copy(src, dst, load_sem.at[n])
        for n, (src, dst) in enumerate(
            ((ids_hbm, ids_ref), (owners_hbm, owners_ref), (feat_hbm, feat))
        )
    ]
    for load in loads:
        load.start()

    def line_peer(j):
        return (y, lax.rem(z + j // ng, nz), x, lax.rem(g + j % ng, ng))

    def plane_peer(j):
        return (lax.rem(y + j // nx, ny), z, lax.rem(x + j % nx, nx), g)

    barrier = pltpu.get_barrier_semaphore()

    @pl.loop(0, reach)
    def _(n):
        peer = lax.rem(me + devices - reach + n, devices)
        pl.semaphore_signal(barrier, 1, device_id=coords(peer, sizes), device_id_type=MESH)

    for j in range(1, line):
        pl.semaphore_signal(barrier, 1, device_id=line_peer(j), device_id_type=MESH)
    for j in range(1, plane):
        pl.semaphore_signal(barrier, 1, device_id=plane_peer(j), device_id_type=MESH)

    loads[0].wait()
    ids = ids_ref[...]
    last = jnp.broadcast_to(ids[tiles - 1 :, TILE - 1 :], (1, TILE))
    in_last = jnp.where(ids == jnp.broadcast_to(last, ids.shape), 1.0, 0.0)
    count = jnp.sum(jnp.sum(in_last, axis=0, keepdims=True), axis=1, keepdims=True)
    first = jnp.broadcast_to(rows_dev - count.astype(jnp.int32), (8, width))
    step = 64
    sub = lax.broadcasted_iota(jnp.int32, (step, width), 0)
    loads[2].wait()

    @pl.loop(0, rows_dev // step, init_carry=jnp.zeros((step, width), jnp.float32), unroll=4)
    def open_rows(t, acc):
        at = pl.ds(pl.multiple_of(t * step, step), step)
        inside = sub + t * step >= jnp.broadcast_to(first[0:1], (step, width))
        return acc + jnp.where(inside, feat[at, :], 0.0)

    total = jnp.sum(open_rows, axis=0, keepdims=True)
    tail[0:1, :] = total[:, :TILE]
    tail[1:2, :] = total[:, TILE:]
    tail[2:3, :] = last.astype(jnp.float32)
    tail[3:4, :] = jnp.broadcast_to(count, (1, TILE))

    loads[1].wait()
    slots = ny * nz * nx * slot_cap
    owners = owners_ref[...]
    across = jnp.broadcast_to(owners, (blocks, blocks))
    down = jnp.broadcast_to(across.T[:, 0:1], (blocks, blocks))
    earlier = lax.broadcasted_iota(jnp.int32, (blocks, blocks), 1) < (
        lax.broadcasted_iota(jnp.int32, (blocks, blocks), 0)
    )
    rank = jnp.sum(jnp.where((across == down) & earlier, 1.0, 0.0), axis=1, keepdims=True)
    target = down[:, 0:1] * slot_cap + rank.astype(jnp.int32)
    hit = jnp.broadcast_to(target, (blocks, slots)) == (
        lax.broadcasted_iota(jnp.int32, (blocks, slots), 1)
    )
    used = jnp.sum(jnp.where(hit, 1.0, 0.0), axis=0, keepdims=True)
    o_from = lax.broadcasted_iota(jnp.int32, (slots, slots), 0)
    o_to = lax.broadcasted_iota(jnp.int32, (slots, slots), 1)

    def plane_of(o):
        return lax.rem(lax.div(o, nx), nz)

    def order_of(o):
        return plane_order(lax.div(o, nx * nz), lax.rem(o, nx), nx)

    ahead = (plane_of(o_from) == plane_of(o_to)) & (order_of(o_from) < order_of(o_to))
    before = jnp.dot(
        jnp.broadcast_to(used, (8, slots)).astype(jnp.bfloat16),
        jnp.where(ahead, 1.0, 0.0).astype(jnp.bfloat16),
        preferred_element_type=jnp.float32,
    )[0:1]
    spot = jnp.where(used > 0.0, before + 1.0, 0.0)
    mine[0:1, :] = spot.astype(jnp.int32)
    home = plane_of(o_to[0:1])
    key = home.astype(jnp.float32) * plane + before

    far = nz // 2
    away = lax.rem(home - z + nz, nz)
    number = [
        jnp.sum(jnp.where(away == d, used, 0.0), axis=1, keepdims=True) for d in range(nz)
    ]
    upper = jnp.floor((number[far] + 1.0) * 0.5)
    listed = jnp.full((1, slots), -1.0, jnp.float32)
    loads_by_hop = []
    for way, shift in ((0, 0.0), (1, 64.0)):
        start = jnp.full((1, 1), shift, jnp.float32)
        starts = []
        for d in range(1, far):
            at = nz - d if way else d
            starts.append(start)
            listed = jnp.where(away == at, before + start, listed)
            start = start + number[at]
        starts.append(start)
        half = (before >= upper) if way else (before < upper)
        skip = upper if way else jnp.zeros_like(upper)
        listed = jnp.where((away == far) & half, before + (start - skip), listed)
        end = start + ((number[far] - upper) if way else upper)
        loads_by_hop.append([end - first for first in starts])
    stats = jnp.zeros((1, slots), jnp.float32)
    hop_lane = lax.broadcasted_iota(jnp.int32, (1, slots), 1)
    for hop in range(far):
        load_here = jnp.maximum(loads_by_hop[0][hop], loads_by_hop[1][hop])
        stats = jnp.where(hop_lane == hop, load_here, stats)
    mine[1:2, :] = stats.astype(jnp.int32)
    list_key = jnp.sum(
        jnp.where(hit, jnp.broadcast_to(listed, (blocks, slots)), 0.0), axis=1, keepdims=True
    )
    block_key = jnp.sum(
        jnp.where(hit, jnp.broadcast_to(key, (blocks, slots)), 0.0), axis=1, keepdims=True
    )
    entry = lax.broadcasted_iota(jnp.int32, (blocks, slots), 1).astype(jnp.float32)
    order = lax.broadcasted_iota(jnp.int32, (blocks, slots), 0)
    for n, one in enumerate((block_key, list_key)):
        pack_out[n : n + 1, :] = jnp.sum(
            jnp.where(jnp.broadcast_to(one, (blocks, slots)) == entry, order, 0),
            axis=0, keepdims=True,
        )

    lane = lax.broadcasted_iota(jnp.int32, ids.shape, 1)
    after = pltpu.roll(ids, TILE - 1, 1)
    end = jnp.where((after != ids) | (lane == TILE - 1), lane, TILE)
    hop = 1
    while hop < TILE:
        nxt = jnp.where(lane + hop < TILE, pltpu.roll(end, TILE - hop, 1), TILE)
        end = jnp.minimum(end, nxt)
        hop *= 2
    ends[...] = end
    prior = jnp.concatenate([jnp.full((1, TILE), -1, jnp.int32), ids[:-1]], axis=0)
    prior = jnp.broadcast_to(prior[:, TILE - 1 :], ids.shape)
    goes_on = jnp.sum(jnp.where(ids == prior, 1.0, 0.0), axis=1, keepdims=True)
    joins[...] = jnp.broadcast_to(goes_on.astype(jnp.int32), ids.shape)

    pl.semaphore_wait(barrier, reach + line - 1 + plane - 1)

    for j in range(1, line):
        pltpu.make_async_remote_copy(
            src_ref=mine, dst_ref=got_line.at[j - 1], send_sem=line_send, recv_sem=line_recv,
            device_id=line_peer(j), device_id_type=MESH,
        ).start()

    @pl.loop(0, reach)
    def _(n):
        k = reach - n
        peer = lax.rem(me + k, devices)
        pltpu.make_async_remote_copy(
            src_ref=tail, dst_ref=got.at[k - 1], send_sem=send_sem, recv_sem=recv_sem,
            device_id=coords(peer, sizes), device_id_type=MESH,
        ).start()

    row = lax.broadcasted_iota(jnp.int32, (TILE, TILE), 0)
    col = lax.broadcasted_iota(jnp.int32, (TILE, TILE), 1)
    causal = col <= row
    ones = jnp.ones((TILE, TILE), jnp.bfloat16)

    @pl.loop(
        0, tiles,
        init_carry=(jnp.zeros((1, width), jnp.float32), jnp.zeros((1, TILE), jnp.float32)),
        unroll=4,
    )
    def _(t, carry):
        open_sum, open_count = carry
        at = pl.ds(pl.multiple_of(t * TILE, TILE), TILE)
        alive = row <= jnp.broadcast_to(ends[pl.ds(t, 1), :], (TILE, TILE))
        mask = jnp.where(alive & causal, 1.0, 0.0).astype(jnp.bfloat16)
        rows = feat[at, :]
        high = rows.astype(jnp.bfloat16)
        rest = rows - high.astype(jnp.float32)
        mid = rest.astype(jnp.bfloat16)
        low = (rest - mid.astype(jnp.float32)).astype(jnp.bfloat16)
        inside = (
            jnp.dot(mask, high, preferred_element_type=jnp.float32)
            + jnp.dot(mask, mid, preferred_element_type=jnp.float32)
            + jnp.dot(mask, low, preferred_element_type=jnp.float32)
        )
        number = jnp.dot(mask, ones, preferred_element_type=jnp.float32)
        joined = row < jnp.broadcast_to(joins[pl.ds(t, 1), :], (TILE, TILE))
        both = jnp.concatenate([joined, joined], axis=1)
        inside = inside + jnp.where(both, jnp.broadcast_to(open_sum, (TILE, width)), 0.0)
        number = number + jnp.where(joined, jnp.broadcast_to(open_count, (TILE, TILE)), 0.0)
        sums[at, :] = inside
        cnt[at, :] = number
        return inside[TILE - 1 :, :], number[TILE - 1 :, :]

    pltpu.make_async_copy(got_line, got_line, line_recv).wait()
    unpack_out[0:1, :] = mine[0:1, :]
    largest = mine[1:2, :]
    for j in range(1, line):
        both = got_line[j - 1]
        largest = jnp.maximum(largest, both[1:2, :])
        if j % ng == 0:
            unpack_out[j // ng : j // ng + 1, :] = both[0:1, :]
    spots = unpack_out[0:nz, :].astype(jnp.float32)
    here = jnp.broadcast_to(plane_of(o_to[0:1]) == z, spots.shape)
    taken = jnp.max(jnp.where(here, spots, 0.0), axis=1, keepdims=True)
    unpack_out[nz : 2 * nz, :] = jnp.broadcast_to(taken, spots.shape).astype(jnp.int32)
    top[...] = largest

    for j in range(1, plane):
        pltpu.make_async_remote_copy(
            src_ref=top, dst_ref=got_plane.at[j - 1], send_sem=plane_send,
            recv_sem=plane_recv, device_id=plane_peer(j), device_id_type=MESH,
        ).start()

    pltpu.make_async_copy(got, got, recv_sem).wait()
    arrived = got[...]
    open_id = arrived[0, 2:3, :]
    age = lax.broadcasted_iota(jnp.int32, arrived.shape, 0) + 1
    same = jnp.broadcast_to(arrived[:, 2:3, :], arrived.shape) == jnp.broadcast_to(
        open_id[None], arrived.shape
    )
    merged = jnp.sum(jnp.where(same & (age <= me), arrived, 0.0), axis=0)
    open_out[0:4, :] = merged
    in_open = jnp.where(
        ids.astype(jnp.float32) == jnp.broadcast_to(open_id, ids.shape), 1.0, 0.0
    )
    reached = jnp.sum(jnp.sum(in_open, axis=0, keepdims=True), axis=1, keepdims=True)
    open_out[4:8, :] = jnp.broadcast_to(reached, (4, TILE))

    pltpu.make_async_copy(got_plane, got_plane, plane_recv).wait()
    for j in range(1, plane):
        largest = jnp.maximum(largest, got_plane[j - 1])
    most_out[...] = largest
    pltpu.make_async_copy(got, got, send_sem).wait()
    pltpu.make_async_copy(got_line, got_line, line_send).wait()
    pltpu.make_async_copy(got_plane, got_plane, plane_send).wait()


def hop_cuts(rooms):
    one, two, three, four = rooms
    ends = ((20, one), (4, 20, two), (4, 8, 12, three), (four,))
    return [list(zip((0,) + cut[:-1], cut)) for cut in ends]


def relay_plan(rooms):
    return [
        (way, hop, a, b)
        for way in (0, 1)
        for hop, cuts in enumerate(hop_cuts(rooms))
        for a, b in cuts
    ]


def exchange_kernel(
    sizes, rooms,
    pack_ref, unpack_ref, sums, cnt, open_ref, out,
    pack, unpack, norm, stage, table_sem, z_send, z_recv, p_send, p_recv, *bufs,
):
    ny, nz, nx, ng = sizes
    plane = ny * nx
    y, z, x, g = place()
    far = nz // 2
    plan = relay_plan(rooms)
    number = {key: n for n, key in enumerate(plan)}
    cuts = hop_cuts(rooms)
    send, recv = bufs[: len(plan)], bufs[len(plan) :]
    barrier = pltpu.get_barrier_semaphore()

    def z_peer(d):
        return (y, lax.rem(z + d, nz), x, g)

    tables = [
        pltpu.make_async_copy(pack_ref, pack, table_sem.at[0]),
        pltpu.make_async_copy(unpack_ref, unpack, table_sem.at[1]),
    ]
    for table in tables:
        table.start()
    for d in (1, nz - 1):
        pl.semaphore_signal(barrier, 1, device_id=z_peer(d), device_id_type=MESH)
    for j in range(1, plane):
        pl.semaphore_signal(
            barrier, 1, device_id_type=MESH,
            device_id=(lax.rem(y + j // nx, ny), z, lax.rem(x + j % nx, nx), g),
        )

    blocks, block_rows, width = norm.shape
    open_sum = jnp.concatenate([open_ref[0:1, :], open_ref[1:2, :]], axis=1)
    open_count = open_ref[3:4, :]
    reached = open_ref[4:5, :].astype(jnp.int32)
    sub = lax.broadcasted_iota(jnp.int32, (block_rows, TILE), 0)

    @pl.loop(0, blocks, unroll=4)
    def _(b):
        at = pl.ds(pl.multiple_of(b * block_rows, block_rows), block_rows)
        joined = sub + b * block_rows < jnp.broadcast_to(reached, (block_rows, TILE))
        count = cnt[at, :] + jnp.where(
            joined, jnp.broadcast_to(open_count, (block_rows, TILE)), 0.0
        )
        scale = 1.0 / jnp.sqrt(count)
        both = jnp.concatenate([joined, joined], axis=1)
        rows = sums[at, :] + jnp.where(
            both, jnp.broadcast_to(open_sum, (block_rows, width)), 0.0
        )
        norm[b] = (rows * jnp.concatenate([scale, scale], axis=1)).astype(jnp.bfloat16)

    for table in tables:
        table.wait()
    for way in (0, 1):
        for a, b in cuts[0]:
            ref = send[number[way, 0, a, b]]

            @pl.loop(0, b - a)
            def _(k):
                ref[k] = norm[pack[1, way * 64 + a + k]]

    pl.semaphore_wait(barrier, 2 + plane - 1)

    def relay(key):
        n = number[key]
        return pltpu.make_async_remote_copy(
            src_ref=send[n], dst_ref=recv[n], send_sem=z_send.at[n], recv_sem=z_recv.at[n],
            device_id=z_peer(nz - 1 if key[0] else 1), device_id_type=MESH,
        )

    def parts(way, hop, count=None):
        return [(recv[number[way, hop, a, b]], a, b) for a, b in cuts[hop][:count]]

    def pick(spot, pieces):
        block = None
        for ref, a, b in pieces:
            one = ref[jnp.clip(spot - 1 - a, 0, b - a - 1)]
            block = one if block is None else jnp.where(spot > a, one, block)
        return block

    def go(hop, piece):
        for way in (0, 1):
            relay((way, hop, *cuts[hop][piece])).start()

    def arrived(hop, piece):
        for way in (0, 1):
            relay((way, hop, *cuts[hop][piece])).wait_recv()

    def repack(hop, piece, count):
        a, b = cuts[hop][piece]
        for way in (0, 1):
            ref = send[number[way, hop, a, b]]
            mine = unpack[nz + (nz - hop if way else hop), 0]
            pieces = parts(way, hop - 1, count)

            @pl.loop(0, b - a)
            def _(k):
                ref[k] = pick(mine + a + k + 1, pieces)

        go(hop, piece)

    def wanted(d, ty, tx, pieces):
        spot = unpack[d, (ty * nz + z) * nx + tx]
        block = pick(spot, pieces)
        return jnp.where(spot > 0, block, jnp.zeros_like(block))

    def wanted_far(ty, tx):
        spot = unpack[far, (ty * nz + z) * nx + tx]
        upper = lax.div(unpack[nz + far, 0] + 1, 2)
        block = jnp.where(
            spot > upper, pick(spot - upper, parts(1, far - 1)), pick(spot, parts(0, far - 1))
        )
        return jnp.where(spot > 0, block, jnp.zeros_like(block))

    def own(ty, tx):
        spot = unpack[0, (ty * nz + z) * nx + tx]
        block = norm[pack[0, z * plane + jnp.maximum(spot, 1) - 1]]
        return jnp.where(spot > 0, block, jnp.zeros_like(block))

    def slot_from(d):
        return (y * nz + lax.rem(z + nz - d, nz)) * nx + x

    def p_copy(d, j, ty, tx):
        return pltpu.make_async_remote_copy(
            src_ref=stage.at[d, j], dst_ref=out.at[slot_from(d)],
            send_sem=p_send, recv_sem=p_recv,
            device_id=(ty, z, tx, g), device_id_type=MESH,
        )

    def deliver(d, block_for):
        def target(j):
            return lax.rem(y + lax.div(j, nx), ny), lax.rem(x + lax.rem(j, nx), nx)

        @pl.loop(1, plane)
        def _(j):
            stage[d, j] = block_for(*target(j))

        @pl.loop(1, plane)
        def _(j):
            p_copy(d, j, *target(j)).start()

        out[slot_from(d)] = block_for(y, x)

    def deliver_from(d, count=None):
        for way in (0, 1):
            step = nz - d if way else d
            pieces = parts(way, d - 1, count)
            deliver(step, lambda ty, tx: wanted(step, ty, tx, pieces))

    def deliver_group(d, group, block_for):
        def target(j):
            ty = lax.rem(y + j, ny)
            return ty, lax.rem(group + ny - ty, nx)

        @pl.loop(0, nx)
        def _(j):
            stage[d, group * nx + j] = block_for(*target(j))

        @pl.loop(0, nx)
        def _(j):
            ty, tx = target(j)

            @pl.when((ty - y) * nx + tx - x != 0)
            def _():
                p_copy(d, group * nx + j, ty, tx).start()

    go(0, 0)
    go(0, 1)
    deliver(0, own)
    arrived(0, 0)
    repack(1, 0, 1)
    deliver_from(1, 1)
    arrived(0, 1)
    repack(1, 1, 2)
    repack(1, 2, 2)
    arrived(1, 0)
    arrived(1, 1)
    repack(2, 0, 2)
    deliver_from(2, 2)
    arrived(1, 2)
    for piece in (1, 2, 3):
        repack(2, piece, 3)
    for group in range(ny):
        arrived(2, group)
        if group == ny - 1:
            repack(3, 0, 4)
        for way in (0, 1):
            step = nz - 3 if way else 3
            pieces = parts(way, 2, group + 1)
            deliver_group(step, group, lambda ty, tx: wanted(step, ty, tx, pieces))
    for way in (0, 1):
        step = nz - 3 if way else 3
        out[slot_from(step)] = wanted(step, y, x, parts(way, 2))
    arrived(3, 0)
    for group in range(ny):
        deliver_group(far, group, wanted_far)
    out[slot_from(far)] = wanted_far(y, x)

    for key in plan:
        relay(key).wait_send()
    landed = out.at[pl.ds(0, nz * (plane - 1))]
    pltpu.make_async_copy(landed, landed, p_send).wait()
    pltpu.make_async_copy(landed, landed, p_recv).wait()


def to_hbm_kernel(src, out, sem):
    parts = sem.shape[0]
    size = src.shape[0] // parts
    copies = [
        pltpu.make_async_copy(
            src.at[pl.ds(n * size, size)], out.at[pl.ds(n * size, size)], sem.at[n]
        )
        for n in range(parts)
    ]
    for copy in copies:
        copy.start()
    for copy in copies:
        copy.wait()


def to_hbm(array):
    return pl.pallas_call(
        to_hbm_kernel,
        out_shape=pltpu.HBM(array.shape, array.dtype),
        in_specs=[pl.BlockSpec(memory_space=pltpu.VMEM)],
        out_specs=pl.BlockSpec(memory_space=pltpu.HBM),
        scratch_shapes=[pltpu.SemaphoreType.DMA((4,))],
        compiler_params=pltpu.CompilerParams(vmem_limit_bytes=1 << 20),
        name="to_hbm",
    )(array)


def body(features, session, owner_map):
    rows_dev, width = features.shape
    blocks = owner_map.shape[1]
    block_rows = rows_dev // blocks
    sizes = tuple(lax.axis_size(name) for name in ROW_GRP)
    ny, nz, nx, ng = sizes
    plane = ny * nx
    slot_cap = max(1, 2 * blocks // (plane * nz))
    slots = plane * nz * slot_cap
    tiles = rows_dev // TILE
    reach = (MOST - 2) // rows_dev + 1
    sums, cnt, open_rows, unpack, pack, most = pl.pallas_call(
        lambda *refs: prelude_kernel(sizes, reach, block_rows, slot_cap, *refs),
        out_shape=(
            jax.ShapeDtypeStruct((rows_dev, width), jnp.float32),
            jax.ShapeDtypeStruct((rows_dev, TILE), jnp.float32),
            jax.ShapeDtypeStruct((8, TILE), jnp.float32),
            jax.ShapeDtypeStruct((2 * nz, slots), jnp.int32),
            jax.ShapeDtypeStruct((2, slots), jnp.int32),
            jax.ShapeDtypeStruct((1, slots), jnp.int32),
        ),
        in_specs=[pl.BlockSpec(memory_space=pltpu.HBM)] * 3,
        out_specs=[pl.BlockSpec(memory_space=pltpu.VMEM)] * 6,
        scratch_shapes=[
            pltpu.VMEM(owner_map.shape, jnp.int32),
            pltpu.VMEM((tiles, TILE), jnp.int32),
            pltpu.VMEM((rows_dev, width), jnp.float32),
            pltpu.VMEM((tiles, TILE), jnp.int32),
            pltpu.VMEM((tiles, TILE), jnp.int32),
            pltpu.VMEM((4, TILE), jnp.float32),
            pltpu.VMEM((reach, 4, TILE), jnp.float32),
            pltpu.VMEM((2, slots), jnp.int32),
            pltpu.VMEM((nz * ng - 1, 2, slots), jnp.int32),
            pltpu.VMEM((1, slots), jnp.int32),
            pltpu.VMEM((plane - 1, 1, slots), jnp.int32),
            pltpu.SemaphoreType.DMA((3,)),
        ]
        + [pltpu.SemaphoreType.DMA] * 6,
        compiler_params=pltpu.CompilerParams(
            collective_id=0, has_side_effects=True, vmem_limit_bytes=24 << 20
        ),
        name="prelude",
    )(
        *(
            pltpu.with_memory_space_constraint(arg, pltpu.HBM)
            for arg in (owner_map, session.reshape(tiles, TILE), features)
        )
    )

    def exchange(room, number):
        block = (block_rows, width)
        return lambda pack, unpack, *rows: to_hbm(pl.pallas_call(
            lambda *refs: exchange_kernel(sizes, room, *refs),
            out_shape=pltpu.VMEM((slots, *block), jnp.bfloat16),
            in_specs=[pl.BlockSpec(memory_space=pltpu.VMEM)] * 5,
            out_specs=pl.BlockSpec(memory_space=pltpu.VMEM),
            scratch_shapes=[
                pltpu.SMEM((2, slots), jnp.int32),
                pltpu.SMEM((2 * nz, slots), jnp.int32),
                pltpu.VMEM((blocks, *block), jnp.bfloat16),
                pltpu.VMEM((nz, plane, *block), jnp.bfloat16),
                pltpu.SemaphoreType.DMA((2,)),
                pltpu.SemaphoreType.DMA((len(relay_plan(room)),)),
                pltpu.SemaphoreType.DMA((len(relay_plan(room)),)),
                pltpu.SemaphoreType.DMA,
                pltpu.SemaphoreType.DMA,
            ]
            + [
                pltpu.VMEM((b - a, *block), jnp.bfloat16)
                for _ in ("send", "recv")
                for _, _, a, b in relay_plan(room)
            ],
            compiler_params=pltpu.CompilerParams(
                collective_id=number, has_side_effects=True, vmem_limit_bytes=32 << 20
            ),
            name=f"exchange_{sum(room)}",
        )(pack, unpack, *rows))

    rooms = ROOMS
    choice = sum(
        jnp.any(most[0, : len(room)] > jnp.array(room)).astype(jnp.int32)
        for room in rooms[:-1]
    )
    return lax.switch(
        choice, [exchange(room, 1 + n) for n, room in enumerate(rooms)],
        pack, unpack, sums, cnt, open_rows,
    )


def solution(mesh):
    split = Mesh(
        mesh.devices.reshape(4, 8, 4, mesh.shape["grp"]), ("row_0", "row_1", "row_2", "grp")
    )
    return jax.shard_map(
        body,
        mesh=split,
        in_specs=(P(ROW_GRP, None), P(ROW_GRP), P(ROW_GRP, None)),
        out_specs=P(ROW_GRP, None, None),
        check_vma=False,
    )
```

profile of v0, /device:TPU:32, one launch (start us, length us, event | category | flops | bytes accessed | tf_op | source)
XLA Modules:
  0.0 109.1 jit_solution(8619476164859702654)
XLA Ops:
  0.0 0.0 copy-start
  0.0 0.0 copy-start.1
  0.0 0.0 copy-start.2
  0.0 0.0 copy-start.3
  0.0 21.4 %prelude.1 = (f32[4096,256]{1,0:T(8,128)}, f32[4096,128]{1,0:T(8,128)S(1)}, f32[8,128]{1,0:T(8,128)S(1)}, s32[16,128]{1,0:T(8,128)S(1)}, s32[2,128]{1,0:T(2,128)S(1)}, /*index=5*/s32[1,128]{1,0:T(1,128)S(1)}) custom-call(s32[1,64]{1,0:T(1,128)} %refs_0_.1, s32[32,128]{1,0:T(8,128)} %bitcast.1, f32[4096,256]{1,0:T(8,128)} %refs_2_.1), custom_call_target="tpu_custom_call" | custom-call | tf_op jit(solution)/shard_map/prelude/pallas_call | solution.py:542
  21.4 0.0 copy-done
  21.4 0.0 copy-done.1
  21.4 0.0 copy-done.2
  21.4 0.0 copy-done.3
  21.4 0.8 compare_reduce_fusion
  24.8 84.4 %conditional.1 = (bf16[128,64,256]{2,1,0:T(8,128)(2,1)}) conditional(s32[]{:T(128)} %clamp.3, (s32[2,128]{1,0:T(2,128)S(1)}, s32[16,128]{1,0:T(8,128)S(1)}, f32[4096,256]{1,0:T(8,128)}, f32[4096,128]{1,0:T(8,128)S(1)}, f32[8,128]{1,0:T(8,128)S(1)}) %tuple.20, (s32[2,128]{1,0:T(2,128)S(1)}, s32[16,128]{1,0:T(8,128)S(1)}, ...), branch_computations={%region_4.0_spmd, %region_5.0_spmd, %region_6.0_spmd, %region_7.0_... | conditional | bytes 8 | solution.py:614
  24.8 82.3 %exchange_91.1.src = bf16[128,64,256]{2,1,0:T(8,128)(2,1)S(1)} custom-call(s32[2,128]{1,0:T(2,128)S(1)} %get-tuple-element.71.refs_0_, s32[16,128]{1,0:T(8,128)S(1)} %get-tuple-element.72.refs_1_, f32[4096,256]{1,0:T(8,128)} %get-tuple-element.73.refs_2_, f32[4096,128]{1,0:T(8,128)S(1)} %get-tuple-element.74.refs_3_, f32[8,128]{1,0:T(8,128)S(1)} %get-tuple-element.75.refs_4_), custom_call_target="tpu_custom_call" | custom-call | tf_op jit(solution)/shard_map/cond/branch_2_fun/exchange_91/pallas_call | solution.py:582
  107.1 2.0 %to_hbm.7 = bf16[128,64,256]{2,1,0:T(8,128)(2,1)} custom-call(bf16[128,64,256]{2,1,0:T(8,128)(2,1)S(1)} %exchange_91.1.src), custom_call_target="tpu_custom_call" | custom-call | tf_op jit(solution)/shard_map/cond/branch_2_fun/to_hbm/pallas_call | solution.py:520
Async XLA Ops:
  0.0 21.4 %copy-start = (s32[1,4]{1,0:T(1,128)S(1)}, s32[1,4]{1,0:T(1,128)}, u32[]{:S(2)}) copy-start(s32[1,4]{1,0:T(1,128)} %constant.22) | copy-start | bytes 52
  0.0 21.4 %copy-start.1 = (s32[1,4]{1,0:T(1,128)S(1)}, s32[1,4]{1,0:T(1,128)}, u32[]{:S(2)}) copy-start(s32[1,4]{1,0:T(1,128)} %constant.21) | copy-start | bytes 52
  0.0 21.4 %copy-start.2 = (s32[1,4]{1,0:T(1,128)S(1)}, s32[1,4]{1,0:T(1,128)}, u32[]{:S(2)}) copy-start(s32[1,4]{1,0:T(1,128)} %constant.20) | copy-start | bytes 52
  0.0 21.4 %copy-start.3 = (s32[1,4]{1,0:T(1,128)S(1)}, s32[1,4]{1,0:T(1,128)}, u32[]{:S(2)}) copy-start(s32[1,4]{1,0:T(1,128)} %constant.19) | copy-start | bytes 52
where the time goes:
time: 110 us; the launch traced here: 109 us
  Pallas kernels  106 us (96%)
  between operations  2.62 us (2%)
    pallas_call x1, Pallas kernels, exchange(): pl.pallas_call(lambda *refs: exchange_kernel(sizes, room, *refs), out_sha...  82.3 us
    pallas_call x1, Pallas kernels, body(): pl.pallas_call(lambda *refs: prelude_kernel(sizes, reach, block_rows, slo...  21.4 us

commit v1 on v0

--- a/solution.py
+++ b/solution.py
@@ -33,7 +33,7 @@
 def prelude_kernel(
     sizes, reach, block_rows, slot_cap,
     owners_hbm, ids_hbm, feat_hbm,
-    sums, cnt, open_out, unpack_out, pack_out, most_out,
+    sums, cnt, open_out, unpack_out, pack_out, choice_out,
     owners_ref, ids_ref, feat, ends, joins, tail, got, mine, got_line, top, got_plane,
     load_sem, send_sem, recv_sem, line_send, line_recv, plane_send, plane_recv,
 ):
@@ -274,7 +274,15 @@
     pltpu.make_async_copy(got_plane, got_plane, plane_recv).wait()
     for j in range(1, plane):
         largest = jnp.maximum(largest, got_plane[j - 1])
-    most_out[...] = largest
+    choice = jnp.zeros((1, 1), jnp.float32)
+    largest = largest.astype(jnp.float32)
+    for rooms in ROOMS[:-1]:
+        room = jnp.zeros((1, slots), jnp.float32)
+        for hop, size in enumerate(rooms):
+            room = jnp.where(hop_lane == hop, float(size), room)
+        over = jnp.max(jnp.where(largest > room, 1.0, 0.0), axis=1, keepdims=True)
+        choice = choice + over
+    choice_out[...] = jnp.broadcast_to(choice, (1, slots)).astype(jnp.int32)
     pltpu.make_async_copy(got, got, send_sem).wait()
     pltpu.make_async_copy(got_line, got_line, line_send).wait()
     pltpu.make_async_copy(got_plane, got_plane, plane_send).wait()
@@ -282,7 +290,7 @@
 
 def hop_cuts(rooms):
     one, two, three, four = rooms
-    ends = ((20, one), (4, 20, two), (4, 8, 12, three), (four,))
+    ends = ((16, 24, one), (8, 12, 20, two), (4, 8, 12, three), (four,))
     return [list(zip((0,) + cut[:-1], cut)) for cut in ends]
 
 
@@ -462,33 +470,45 @@
             def _():
                 p_copy(d, group * nx + j, ty, tx).start()
 
-    go(0, 0)
-    go(0, 1)
+    def deliver_groups(d, groups, count):
+        for way in (0, 1):
+            step = nz - d if way else d
+            pieces = parts(way, d - 1, count)
+            for group in groups:
+                deliver_group(step, group, lambda ty, tx: wanted(step, ty, tx, pieces))
+
+    def keep(d):
+        for way in (0, 1):
+            step = nz - d if way else d
+            out[slot_from(step)] = wanted(step, y, x, parts(way, d - 1))
+
+    for piece in range(3):
+        go(0, piece)
     deliver(0, own)
     arrived(0, 0)
-    repack(1, 0, 1)
     deliver_from(1, 1)
     arrived(0, 1)
-    repack(1, 1, 2)
-    repack(1, 2, 2)
+    repack(1, 0, 2)
+    arrived(0, 2)
+    for piece in (1, 2, 3):
+        repack(1, piece, 3)
     arrived(1, 0)
+    deliver_groups(2, (0, 1), 1)
     arrived(1, 1)
-    repack(2, 0, 2)
-    deliver_from(2, 2)
+    deliver_groups(2, (2,), 2)
     arrived(1, 2)
+    repack(2, 0, 3)
+    deliver_groups(2, (3,), 3)
+    arrived(1, 3)
     for piece in (1, 2, 3):
-        repack(2, piece, 3)
+        repack(2, piece, 4)
+    keep(2)
     for group in range(ny):
         arrived(2, group)
         if group == ny - 1:
             repack(3, 0, 4)
-        for way in (0, 1):
-            step = nz - 3 if way else 3
-            pieces = parts(way, 2, group + 1)
-            deliver_group(step, group, lambda ty, tx: wanted(step, ty, tx, pieces))
-    for way in (0, 1):
-        step = nz - 3 if way else 3
-        out[slot_from(step)] = wanted(step, y, x, parts(way, 2))
+        deliver_groups(3, (group,), group + 1)
+    keep(3)
     arrived(3, 0)
     for group in range(ny):
         deliver_group(far, group, wanted_far)
@@ -539,7 +559,7 @@
     slots = plane * nz * slot_cap
     tiles = rows_dev // TILE
     reach = (MOST - 2) // rows_dev + 1
-    sums, cnt, open_rows, unpack, pack, most = pl.pallas_call(
+    sums, cnt, open_rows, unpack, pack, choice = pl.pallas_call(
         lambda *refs: prelude_kernel(sizes, reach, block_rows, slot_cap, *refs),
         out_shape=(
             jax.ShapeDtypeStruct((rows_dev, width), jnp.float32),
@@ -601,18 +621,14 @@
                 for _, _, a, b in relay_plan(room)
             ],
             compiler_params=pltpu.CompilerParams(
-                collective_id=number, has_side_effects=True, vmem_limit_bytes=32 << 20
+                collective_id=number, has_side_effects=True, vmem_limit_bytes=24 << 20
             ),
             name=f"exchange_{sum(room)}",
         )(pack, unpack, *rows))
 
     rooms = ROOMS
-    choice = sum(
-        jnp.any(most[0, : len(room)] > jnp.array(room)).astype(jnp.int32)
-        for room in rooms[:-1]
-    )
     return lax.switch(
-        choice, [exchange(room, 1 + n) for n, room in enumerate(rooms)],
+        choice[0, 0], [exchange(room, 1 + n) for n, room in enumerate(rooms)],
         pack, unpack, sums, cnt, open_rows,
     )
 

time: 110 us -> 101 us (0.918)
  Pallas kernels: 106 us -> 99.5 us
  between operations: 2.62 us -> 0.04 us
    pallas_call x1, Pallas kernels: 82.3 us -> 78.2 us  [exchange(): pl.pallas_call(lambda *refs: exchange_kernel(sizes, room, *refs), out_sha...]
    pallas_call x1, Pallas kernels: 21.4 us -> 19.2 us  [body(): pl.pallas_call(lambda *refs: prelude_kernel(sizes, reach, block_rows, slo...]
where the time goes in v1:
time: 101 us; the launch traced here: 99.5 us
  Pallas kernels  99.5 us (99%)
    pallas_call x1, Pallas kernels, exchange(): pl.pallas_call(lambda *refs: exchange_kernel(sizes, room, *refs), out_sha...  78.2 us
    pallas_call x1, Pallas kernels, body(): pl.pallas_call(lambda *refs: prelude_kernel(sizes, reach, block_rows, slo...  19.2 us
    pallas_call x1, Pallas kernels, to_hbm(): pl.pallas_call(to_hbm_kernel, out_shape=pltpu.HBM(array.shape, array.dtyp...  2.04 us

profile of v1, /device:TPU:32, one launch (start us, length us, event | category | flops | bytes accessed | tf_op | source)
XLA Modules:
  0.0 99.5 jit_solution(13498842378031365037)
XLA Ops:
  0.0 19.2 %prelude.1 = (f32[4096,256]{1,0:T(8,128)S(1)}, f32[4096,128]{1,0:T(8,128)S(1)}, f32[8,128]{1,0:T(8,128)S(1)}, s32[16,128]{1,0:T(8,128)S(1)}, s32[2,128]{1,0:T(2,128)S(1)}, /*index=5*/s32[1,128]{1,0:T(1,128)S(1)}) custom-call(s32[1,64]{1,0:T(1,128)} %refs_0_.1, s32[32,128]{1,0:T(8,128)} %bitcast.4, f32[4096,256]{1,0:T(8,128)} %refs_2_.1), custom_call_target="tpu_custom_call" | custom-call | tf_op jit(solution)/shard_map/prelude/pallas_call | solution.py:562
  19.2 80.3 %conditional.1 = (bf16[128,64,256]{2,1,0:T(8,128)(2,1)}) conditional(s32[]{:T(128)} %bitcast.1, (s32[2,128]{1,0:T(2,128)S(1)}, s32[16,128]{1,0:T(8,128)S(1)}, f32[4096,256]{1,0:T(8,128)S(1)}, f32[4096,128]{1,0:T(8,128)S(1)}, f32[8,128]{1,0:T(8,128)S(1)}) %tuple.20, (s32[2,128]{1,0:T(2,128)S(1)}, ...), branch_computations={%region_0.0_spmd, %region_1.0_spmd, %region_2.0_spmd, %region_3.0_... | conditional | bytes 8 | solution.py:630
  19.2 78.2 %exchange_88.1.src = bf16[128,64,256]{2,1,0:T(8,128)(2,1)S(1)} custom-call(s32[2,128]{1,0:T(2,128)S(1)} %get-tuple-element.66.refs_0_, s32[16,128]{1,0:T(8,128)S(1)} %get-tuple-element.67.refs_1_, f32[4096,256]{1,0:T(8,128)S(1)} %get-tuple-element.68.refs_2_, f32[4096,128]{1,0:T(8,128)S(1)} %get-tuple-element.69.refs_3_, f32[8,128]{1,0:T(8,128)S(1)} %get-tuple-element.70.refs_4_), custom_call_target="tpu_custom_call" | custom-call | tf_op jit(solution)/shard_map/cond/branch_1_fun/exchange_88/pallas_call | solution.py:602
  97.5 2.0 %to_hbm.6 = bf16[128,64,256]{2,1,0:T(8,128)(2,1)} custom-call(bf16[128,64,256]{2,1,0:T(8,128)(2,1)S(1)} %exchange_88.1.src), custom_call_target="tpu_custom_call" | custom-call | tf_op jit(solution)/shard_map/cond/branch_1_fun/to_hbm/pallas_call | solution.py:540
